TPU v7x, 256 devices: a whole 4x4x8 slice. The times are simulated.
256 devices in a mesh: fsdp: 64 (over y, z, core), refresh: 4 (over x).
Axes of the slice: x: 4, y: 4, z: 8, core: 2. Of those that a mesh axis runs over, the one named last changes fastest.
Arguments:
- gradient: bfloat16 [4, 192, 65536], P('refresh', None, 'fsdp'), may hold values from -6 to 6
- owner: int32 [4, 192, 1], P('refresh'), may hold values from 0 to 63; in each aligned block of 192 rows (0 to 191, 192 to 383, ..., all dimensions but the last counted through in order) at most 4 rows name the same one
- rotation: int32 [64], replicated, may hold values from 0 to 3
- left_factor: float32 [4, 256, 256, 256], P('refresh', 'fsdp'), may hold values from -1 to 8, as said below
- right_factor: float32 [4, 256, 256, 256], P('refresh', 'fsdp'), may hold values from -1 to 8, as said below
- left_basis: float32 [4, 256, 256, 256], P('refresh', 'fsdp'), may hold values from -1 to 1, as said below
- right_basis: float32 [4, 256, 256, 256], P('refresh', 'fsdp'), may hold values from -1 to 1, as said below
- moment: float32 [4, 256, 256, 256], P('refresh', 'fsdp'), may hold values from -4 to 4
- second_moment: float32 [4, 256, 256, 256], P('refresh', 'fsdp'), may hold values from 0.05 to 2
Outputs:
- direction: float32 [4, 192, 65536], P('refresh', None, 'fsdp')
- left_factor_new: float32 [4, 256, 256, 256], P('refresh', 'fsdp')
- right_factor_new: float32 [4, 256, 256, 256], P('refresh', 'fsdp')
- left_basis_new: float32 [4, 256, 256, 256], P('refresh', 'fsdp')
- right_basis_new: float32 [4, 256, 256, 256], P('refresh', 'fsdp')
- moment_new: float32 [4, 256, 256, 256], P('refresh', 'fsdp')
- second_moment_new: float32 [4, 256, 256, 256], P('refresh', 'fsdp')
Inputs may be any that keep to these rules, and one draw needn't show every extreme that they name: Within each group no owner is named by more than 4 blocks, a bound that some block reaches; some owner is named by at least one block. The state of block b lies in slot s(b) of the steps; the states of slots that no block takes are carried unchanged. `left_factor`: each slot's factor is symmetric positive definite. `right_factor`: each slot's factor is symmetric positive definite. `left_basis`: each slot's basis is orthogonal. `right_basis`: each slot's basis is orthogonal.
All inputs are finite; a program needn't handle non-finite values.
Results may differ from a plain program's by a relative error of at most 0.0003.
Values may be sent and summed in bfloat16 or wider, within the bound.
No kernel may reach another device: no remote copies, remote signals or barrier semaphores. Data moves between devices by JAX's collectives and lax.ppermute only.
A program may use at most 64 MiB of HBM per device.

v0:
```python
import jax
import jax.numpy as jnp
from jax import lax
from jax.sharding import PartitionSpec as P

HIGHEST = lax.Precision.HIGHEST
EPSILON = 1e-08


def split_up(value, dim, length):
    before, after = (value.shape[:dim], value.shape[dim + 1 :])
    return jnp.moveaxis(value.reshape(*before, length, -1, *after), dim, 0)


def sum_at_owner(value, axis, dim):
    blocks = split_up(value, dim, lax.axis_size(axis))
    arrived = lax.all_to_all(blocks, axis, split_axis=0, concat_axis=0, tiled=True)
    return arrived.sum(axis=0)


def image_of(factor, basis):
    return jnp.einsum("sij,sjk->sik", factor, basis, precision=HIGHEST)


def finish_step(image):
    gram = jnp.einsum("sji,sjk->sik", image, image, precision=HIGHEST)
    lower = jnp.linalg.cholesky(gram)
    solved = jax.scipy.linalg.solve_triangular(lower, jnp.swapaxes(image, 1, 2), lower=True)
    return jnp.swapaxes(solved, 1, 2)


def rotate_pair(left, middle, right):
    inner = jnp.einsum("sji,sjk->sik", left, middle, precision=HIGHEST)
    return jnp.einsum("sij,sjk->sik", inner, right, precision=HIGHEST)


def body(
    gradient,
    owner,
    rotation,
    left_factor,
    right_factor,
    left_basis,
    right_basis,
    moment,
    second_moment,
):
    shards = lax.axis_size("fsdp")
    helpers = lax.axis_size("refresh")
    mine = lax.axis_index("fsdp")
    group = lax.axis_index("refresh")
    cap = left_factor.shape[1]
    width = left_factor.shape[2]
    owners = owner[0, :, 0]
    onehot = (owners[:, None] == jnp.arange(shards, dtype=jnp.int32)[None, :]).astype(jnp.int32)
    before = jnp.cumsum(onehot, axis=0) - onehot
    target = owners * cap + jnp.sum(before * onehot, axis=1)
    placing = (target[None, :] == jnp.arange(shards * cap, dtype=jnp.int32)[:, None]).astype(
        jnp.bfloat16
    )
    outgoing = jnp.dot(placing, gradient[0], preferred_element_type=jnp.float32).astype(
        jnp.bfloat16
    )
    arrived = lax.all_to_all(outgoing, "fsdp", split_axis=0, concat_axis=1, tiled=True)
    blocks = arrived.reshape(cap, width, width)
    count = jnp.sum((owners == mine).astype(jnp.int32))
    keep = (jnp.arange(cap, dtype=jnp.int32) < count)[:, None, None]
    left_old = left_factor[0]
    right_old = right_factor[0]
    left_turn = left_basis[0]
    right_turn = right_basis[0]
    gram_left = jnp.einsum("sij,skj->sik", blocks, blocks, preferred_element_type=jnp.float32)
    gram_right = jnp.einsum("sji,sjk->sik", blocks, blocks, preferred_element_type=jnp.float32)
    left_new = 0.95 * left_old + 0.05 / width * gram_left
    right_new = 0.95 * right_old + 0.05 / width * gram_right
    wide = blocks.astype(jnp.float32)
    moment_next = 0.9 * moment[0] + 0.1 * wide
    turned = rotate_pair(left_turn, wide, right_turn)
    turned_moment = rotate_pair(left_turn, moment_next, right_turn)
    second_next = 0.95 * second_moment[0] + 0.05 * turned * turned
    scaled = turned_moment / (jnp.sqrt(second_next) + EPSILON)
    backed = jnp.einsum("sij,sjk->sik", left_turn, scaled, precision=HIGHEST)
    update = jnp.einsum("sij,skj->sik", backed, right_turn, precision=HIGHEST)
    returned = lax.all_to_all(
        update.reshape(cap, width * width), "fsdp", split_axis=1, concat_axis=0, tiled=True
    )
    direction = jnp.take(returned, target, axis=0)
    factors = jnp.stack([left_new[0], right_new[0]], axis=0)
    bases = jnp.stack([left_turn[0], right_turn[0]], axis=0)
    chosen = lax.dynamic_index_in_dim(rotation, mine, 0, keepdims=False)
    share_count = -(-2 // helpers)
    extra = share_count * helpers - 2
    filler = jnp.broadcast_to(jnp.eye(width, dtype=jnp.float32), (extra, width, width))
    images_all = jnp.concatenate([image_of(factors, bases), filler], axis=0)
    offered = jnp.where(group == chosen, images_all, jnp.zeros_like(images_all))
    received = sum_at_owner(offered, "refresh", 0)
    fresh = lax.all_gather(finish_step(received), "refresh", axis=0, tiled=True)[:2]
    leading = (jnp.arange(cap, dtype=jnp.int32) == 0)[:, None, None]
    refreshed = keep & leading & (group == chosen)
    left_basis_new = jnp.where(refreshed, fresh[0][None], left_turn)
    right_basis_new = jnp.where(refreshed, fresh[1][None], right_turn)
    return (
        direction[None],
        jnp.where(keep, left_new, left_old)[None],
        jnp.where(keep, right_new, right_old)[None],
        left_basis_new[None],
        right_basis_new[None],
        jnp.where(keep, moment_next, moment[0])[None],
        jnp.where(keep, second_next, second_moment[0])[None],
    )


def solution(mesh):
    in_specs = (
        P("refresh", None, "fsdp"),
        P("refresh", None, None),
        P(),
        P("refresh", "fsdp", None, None),
        P("refresh", "fsdp", None, None),
        P("refresh", "fsdp", None, None),
        P("refresh", "fsdp", None, None),
        P("refresh", "fsdp", None, None),
        P("refresh", "fsdp", None, None),
    )
    out_specs = (
        P("refresh", None, "fsdp"),
        P("refresh", "fsdp", None, None),
        P("refresh", "fsdp", None, None),
        P("refresh", "fsdp", None, None),
        P("refresh", "fsdp", None, None),
        P("refresh", "fsdp", None, None),
        P("refresh", "fsdp", None, None),
    )
    return jax.shard_map(body, mesh=mesh, in_specs=in_specs, out_specs=out_specs, check_vma=False)
```

profile of v0, /device:TPU:8, one launch (start us, length us, event | category | flops | bytes accessed | tf_op | source)
XLA Modules:
  0.0 189.4 jit_solution(3342980316965750241)
XLA Ops:
  7.2 0.7 copy-done.21
  9.3 1.0 all_to_all.29
  10.2 12.2 %all-to-all-start = ((bf16[64,4,1024]{2,1,0:T(4,128)(2,1)}), bf16[64,4,1024]{2,1,0:T(4,128)(2,1)S(1)}, u32[]{:S(2)}, u32[]{:S(2)}) async-start(bf16[64,4,1024]{2,1,0:T(4,128)(2,1)} %all_to_all.29), calls=%async_computation | async-start | bytes 1048576 | tf_op jit(solution)/shard_map/all_to_all | solution.py:64
  26.4 0.7 slice_bitcast_fusion.3
  27.1 0.7 slice_bitcast_fusion.2
  27.9 11.3 %all-to-all-done = bf16[64,4,1024]{2,1,0:T(4,128)(2,1)S(1)} async-done(((bf16[64,4,1024]{2,1,0:T(4,128)(2,1)}), bf16[64,4,1024]{2,1,0:T(4,128)(2,1)S(1)}, u32[]{:S(2)}, u32[]{:S(2)}) %all-to-all-start) | async-done | bytes 524320 | tf_op jit(solution)/shard_map/all_to_all | solution.py:64
  39.2 1.0 copy.114
  40.1 1.4 reshape.256
  41.5 2.0 %fusion.17 = f32[4,256,256]{1,2,0:T(8,128)} fusion(bf16[4,256,256]{2,1,0:T(8,128)(2,1)S(1)} %reshape.256, f32[1,4,256,256]{3,2,1,0:T(8,128)S(1)} %copy-done.1), kind=kOutput, calls=%fused_computation.33 | convolution fusion | flops 805306368 | bytes 2621440 | tf_op jit(solution)/shard_map/sji,sjk->sik/dot_general | solution.py:33
  43.9 0.8 copy-done.9
  45.2 1.1 copy-done.14
  47.5 1.1 fusion.4
  48.6 4.4 %all-to-all-start.2 = ((f32[4,1,256,256]{3,2,1,0:T(8,128)}), f32[4,1,256,256]{3,2,1,0:T(8,128)}, u32[]{:S(2)}, u32[]{:S(2)}) async-start(f32[4,1,256,256]{3,2,1,0:T(8,128)} %fusion.4), calls=%async_computation.2 | async-start | bytes 2097152 | tf_op jit(solution)/shard_map/all_to_all | solution.py:17
  53.1 3.3 %fusion.19 = f32[4,256,256]{1,2,0:T(8,128)S(1)} fusion(f32[1,4,256,256]{3,2,1,0:T(8,128)S(1)} %copy-done.1, bf16[4,256,256]{2,1,0:T(8,128)(2,1)S(1)} %reshape.256, f32[1,4,256,256]{3,2,1,0:T(8,128)} %param.16), kind=kOutput, calls=%fused_computation.35 | convolution fusion | flops 806354944 | bytes 3670016 | tf_op jit(solution)/shard_map/sji,sjk->sik/dot_general | solution.py:33
  56.4 1.3 fusion.3
  57.7 1.4 convolution_divide_fusion
  59.1 1.2 fusion.15
  60.2 2.1 %fusion.8 = f32[4,256,256]{2,1,0:T(8,128)} fusion(f32[4,256,256]{1,2,0:T(8,128)S(1)} %fusion.15, f32[1,4,256,256]{3,2,1,0:T(8,128)S(1)} %copy-done.2), kind=kOutput, calls=%fused_computation.26 | convolution fusion | flops 805306368 | bytes 3145728 | tf_op jit(solution)/shard_map/sij,skj->sik/dot_general | solution.py:83
  62.4 2.5 %all_to_all.32 = f32[4,64,1024]{2,1,0:T(8,128)} reshape(f32[4,256,256]{2,1,0:T(8,128)} %fusion.8) | data formatting | bytes 2097152 | tf_op jit(solution)/shard_map/all_to_all | solution.py:84
  64.8 2.9 %copy.92 = f32[4,64,1024]{2,0,1:T(4,128)} copy(f32[4,64,1024]{2,1,0:T(8,128)} %all_to_all.32) | data formatting | bytes 2097152 | tf_op jit(solution)/shard_map/all_to_all | solution.py:84
  67.7 1.4 all-to-all-done.2
  69.1 6.3 %all-to-all-start.1 = ((f32[4,64,1024]{2,0,1:T(4,128)}), f32[4,64,1024]{2,0,1:T(4,128)}, u32[]{:S(2)}, u32[]{:S(2)}) async-start(f32[4,64,1024]{2,0,1:T(4,128)} %copy.92), calls=%async_computation.1 | async-start | bytes 2097152 | tf_op jit(solution)/shard_map/all_to_all | solution.py:84
  75.7 1.3 reduce_sum.34
  77.6 0.8 copy.97
  79.3 11.7 %custom-call.17 = f32[1,128,128]{2,1,0:T(8,128)S(1)} custom-call(f32[1,128,128]{2,1,0:T(8,128)S(1)} %cholesky.117), custom_call_target="Cholesky" | custom-call | tf_op jit(solution)/shard_map/jit(cholesky)/cholesky | solution.py:27
  92.3 0.9 cholesky.111
  93.2 11.3 %custom-call.18 = f32[1,1,128,128]{2,3,1,0:T(8,128)} custom-call(f32[1,1,128,128]{3,2,1,0:T(8,128)} %get-tuple-element.39), custom_call_target="InvertDiagBlocksLowerTriangular" | custom-call | tf_op jit(solution)/shard_map/jit(cholesky)/cholesky | solution.py:27
  104.5 1.0 bitcast_dynamic-update-slice_fusion.1
  105.5 0.9 fusion.2
  106.4 12.5 %custom-call.19 = f32[1,128,128]{2,1,0:T(8,128)S(1)} custom-call(f32[1,128,128]{2,1,0:T(8,128)} %fusion.2), custom_call_target="Cholesky" | custom-call | tf_op jit(solution)/shard_map/jit(cholesky)/cholesky | solution.py:27
  121.7 5.2 %while.1 = (s32[]{:T(128)}, f32[256,256]{1,0:T(8,128)S(1)}, s32[2,2]{1,0:T(2,128)S(1)}, f32[2,128,128]{2,1,0:T(8,128)}, s32[]{:T(128)}) while((s32[]{:T(128)}, f32[256,256]{1,0:T(8,128)S(1)}, s32[2,2]{1,0:T(2,128)S(1)}, f32[2,128,128]{2,1,0:T(8,128)}, s32[]{:T(128)}) %tuple.33), condition=%wide.while_cond, body=%wide.while_body.sunk | while | flops 2 | bytes 132205 | solution.py:28
  122.3 2.0 %bitcast_dynamic-update-slice_fusion.3 = f32[2,128,128]{2,1,0:T(8,128)} fusion(f32[2,128,128]{2,1,0:T(8,128)} %get-tuple-element.86, s32[]{:T(128)S(6)} %copy.120, f32[256,256]{1,0:T(8,128)S(1)} %get-tuple-element.89, s32[]{:T(128)} %bitcast.158, s32[]{:T(128)} %bitcast.159), kind=kLoop, calls=%fused_computation.1.clone.1 | loop fusion | bytes 132100 | tf_op jit(solution)/shard_map/jit(_solve_triangular)/triangular_solve
  124.9 2.0 %bitcast_dynamic-update-slice_fusion.3 = f32[2,128,128]{2,1,0:T(8,128)} fusion(f32[2,128,128]{2,1,0:T(8,128)} %get-tuple-element.86, s32[]{:T(128)S(6)} %copy.120, f32[256,256]{1,0:T(8,128)S(1)} %get-tuple-element.89, s32[]{:T(128)} %bitcast.158, s32[]{:T(128)} %bitcast.159), kind=kLoop, calls=%fused_computation.1.clone.1 | loop fusion | bytes 132100 | tf_op jit(solution)/shard_map/jit(_solve_triangular)/triangular_solve
  126.9 20.5 %custom-call.20 = f32[2,128,128]{1,2,0:T(8,128)S(1)} custom-call(f32[2,128,128]{2,1,0:T(8,128)} %get-tuple-element.14), custom_call_target="InvertDiagBlocksLowerTriangular" | custom-call | tf_op jit(solution)/shard_map/jit(_solve_triangular)/triangular_solve | solution.py:28
  148.0 1.2 fusion.35
  149.3 1.2 convolution_subtract_fusion
  150.8 0.8 copy.98
  152.4 1.2 and_and_fusion
  153.6 1.2 convert_multiply_fusion
  154.8 2.5 %mul.104 = f32[1,4,256,256]{3,2,1,0:T(8,128)} reshape(f32[4,64,1024]{2,1,0:T(8,128)} %convert_multiply_fusion) | data formatting | bytes 2097152 | tf_op jit(solution)/shard_map/mul | solution.py:77
  157.3 2.9 %add_select_fusion = f32[1,4,256,256]{3,2,1,0:T(8,128)} fusion(f32[1,4,256,256]{3,2,1,0:T(8,128)} %param.16, f32[1,4,256,256]{3,2,1,0:T(8,128)} %mul.104, pred[4]{0:T(512)(128)(4,1)S(1)} %iota_compare_fusion.9), kind=kLoop, calls=%fused_computation.38 | loop fusion | flops 786432 | bytes 3145732 | tf_op jit(solution)/shard_map/jit(_where)/select_n | solution.py:108
  160.2 3.7 %fusion.7 = (f32[1,4,256,256]{3,2,1,0:T(8,128)}, f32[1,4,256,256]{3,2,1,0:T(8,128)}, f32[1,4,256,256]{3,2,1,0:T(8,128)}) fusion(f32[4,256,256]{2,1,0:T(8,128)} %copy-done.11, f32[1,4,256,256]{3,2,1,0:T(8,128)} %param.17, pred[4]{0:T(512)(128)(4,1)S(1)} %iota_compare_fusion.9, f32[4,256,256]{2,1,0:T(8,128)S(1)} %copy-done.4, ...), kind=kLoop, calls=%fused_computation.25 | loop fusion | flops 786432 | bytes 9437188 | tf_op jit(solution)/shard_map/broadcast_in_dim | solution.py:109
  163.9 1.6 all_to_all.35
  165.5 1.8 gather_fusion
  167.3 2.1 %bitcast_select_fusion.3 = f32[1,192,1024]{2,1,0:T(8,128)} fusion(f32[192,1024]{1,0:T(8,128)} %gather_fusion, pred[192]{0:T(512)(128)(4,1)S(1)} %get-tuple-element.30), kind=kLoop, calls=%fused_computation.43 | loop fusion | flops 196608 | bytes 1573056 | tf_op jit(solution)/shard_map/jit(_take)/select_n | solution.py:87
  169.5 9.8 %all-gather.2.cloned.1.call-done = f32[4,256,256]{2,1,0:T(8,128)} async-done(((f32[1,256,256]{2,1,0:T(8,128)}), f32[4,256,256]{2,1,0:T(8,128)}) %all-gather.2.cloned.1.call-update) | async-done | bytes 1048592 | tf_op jit(solution)/shard_map/all_gather | solution.py:97
  179.3 1.1 slice_bitcast_fusion
  181.0 1.6 broadcast_select_fusion
  (89 shorter events, 14.4 us)
Async XLA Ops:
  7.2 1.8 copy-start
  7.2 0.7 copy-start.21
  9.2 17.2 %copy-start.1 = (f32[1,4,256,256]{3,2,1,0:T(8,128)S(1)}, f32[1,4,256,256]{3,2,1,0:T(8,128)}, u32[]{:S(2)}) copy-start(f32[1,4,256,256]{3,2,1,0:T(8,128)} %param.14) | copy-start | bytes 3145732
  10.2 16.9 %copy-start.2 = (f32[1,4,256,256]{3,2,1,0:T(8,128)S(1)}, f32[1,4,256,256]{3,2,1,0:T(8,128)}, u32[]{:S(2)}) copy-start(f32[1,4,256,256]{3,2,1,0:T(8,128)} %param.15) | copy-start | bytes 3145732
  10.2 28.9 %all-to-all-start = ((bf16[64,4,1024]{2,1,0:T(4,128)(2,1)}), bf16[64,4,1024]{2,1,0:T(4,128)(2,1)S(1)}, u32[]{:S(2)}, u32[]{:S(2)}) async-start(bf16[64,4,1024]{2,1,0:T(4,128)(2,1)} %all_to_all.29), calls=%async_computation | async-start | bytes 1048576 | tf_op jit(solution)/shard_map/all_to_all | solution.py:64
  22.5 0.7 copy-start.23
  41.5 2.0 %copy-start.7 = (f32[1,4,256,256]{3,2,1,0:T(8,128)S(1)}, f32[1,4,256,256]{3,2,1,0:T(8,128)}, u32[]{:S(2)}) copy-start(f32[1,4,256,256]{3,2,1,0:T(8,128)} %param.13) | copy-start | bytes 3145732
  43.5 1.2 copy-start.9
  43.9 1.2 copy-start.3
  45.1 2.1 %copy-start.5 = (f32[4,256,256]{2,1,0:T(8,128)}, f32[4,256,256]{2,1,0:T(8,128)S(1)}, u32[]{:S(2)}) copy-start(f32[4,256,256]{2,1,0:T(8,128)S(1)} %fusion.1) | copy-start | bytes 3145732
  45.1 1.1 copy-start.14
  45.1 1.4 copy-start.15
  46.5 0.9 copy-start.13
  48.6 20.5 %all-to-all-start.2 = ((f32[4,1,256,256]{3,2,1,0:T(8,128)}), f32[4,1,256,256]{3,2,1,0:T(8,128)}, u32[]{:S(2)}, u32[]{:S(2)}) async-start(f32[4,1,256,256]{3,2,1,0:T(8,128)} %fusion.4), calls=%async_computation.2 | async-start | bytes 2097152 | tf_op jit(solution)/shard_map/all_to_all | solution.py:17
  53.0 3.3 %copy-start.10 = (f32[1,4,256,256]{3,2,1,0:T(8,128)S(1)}, f32[1,4,256,256]{3,2,1,0:T(8,128)}, u32[]{:S(2)}) copy-start(f32[1,4,256,256]{3,2,1,0:T(8,128)} %param.17) | copy-start | bytes 3145732
  53.1 3.3 %copy-start.12 = (f32[4,256,256]{1,2,0:T(8,128)S(1)}, f32[4,256,256]{1,2,0:T(8,128)}, u32[]{:S(2)}) copy-start(f32[4,256,256]{1,2,0:T(8,128)} %fusion.17) | copy-start | bytes 3145732
  57.6 1.4 copy-start.11
  69.1 94.8 %all-to-all-start.1 = ((f32[4,64,1024]{2,0,1:T(4,128)}), f32[4,64,1024]{2,0,1:T(4,128)}, u32[]{:S(2)}, u32[]{:S(2)}) async-start(f32[4,64,1024]{2,0,1:T(4,128)} %copy.92), calls=%async_computation.1 | async-start | bytes 2097152 | tf_op jit(solution)/shard_map/all_to_all | solution.py:84
  75.4 103.9 %all-gather.2.cloned.1.call-start = ((), (), s32[]{:S(2)}) async-start(), calls=%async_computation.3 | async-start | bytes 1310720 | tf_op jit(solution)/shard_map/all_gather | solution.py:97
  78.6 0.7 copy-start.16
  79.3 25.1 %copy-start.17 = (f32[1,256,256]{2,1,0:T(8,128)S(1)}, f32[1,256,256]{2,1,0:T(8,128)}, u32[]{:S(2)}) copy-start(f32[1,256,256]{2,1,0:T(8,128)} %copy-done.16) | copy-start | bytes 786436
  91.1 0.6 copy-start.18
  120.9 0.7 copy-start.24
  147.4 0.7 copy-start.19
  149.3 1.2 copy-start.20
  157.3 2.9 %copy-start.4 = (f32[4,256,256]{2,1,0:T(8,128)S(1)}, f32[4,256,256]{2,1,0:T(8,128)}, u32[]{:S(2)}) copy-start(f32[4,256,256]{2,1,0:T(8,128)} %copy-done.3) | copy-start | bytes 3145732
  157.3 2.9 %copy-start.6 = (f32[4,256,256]{2,1,0:T(8,128)S(1)}, f32[4,256,256]{2,1,0:T(8,128)}, u32[]{:S(2)}) copy-start(f32[4,256,256]{2,1,0:T(8,128)} %copy-done.5) | copy-start | bytes 3145732
  157.3 2.9 %copy-start.8 = (f32[1,4,256,256]{3,2,1,0:T(8,128)S(1)}, f32[1,4,256,256]{3,2,1,0:T(8,128)}, u32[]{:S(2)}) copy-start(f32[1,4,256,256]{3,2,1,0:T(8,128)} %param.13) | copy-start | bytes 3145732
  180.4 0.6 copy-start.22
Sparse Core Ops, SparseCore 0:
  151.8 27.4 all-gather.1
where the time goes:
time: 191 us; the launch traced here: 189 us
  other arithmetic  76.1 us (40%)
  local copies, waits for them, and re-layouts  33 us (17%)
  starting transfers between devices  23.3 us (12%)
  waiting for transfers between devices  22.5 us (12%)
  matrix products  18.1 us (9%)
  between operations  16.5 us (9%)
    another operation x6, other arithmetic, finish_step(): lower = jnp.linalg.cholesky(gram)  36.8 us
    another operation x3, other arithmetic, finish_step(): jax.scipy.linalg.solve_triangular(lower, jnp.swapaxes(image, 1, 2), lower...  21.1 us
    all_to_all x1, starting transfers between devices, body(): lax.all_to_all(outgoing, 'fsdp', split_axis=0, concat_axis=1, tiled=True)  12.2 us
    all_to_all x1, waiting for transfers between devices, body(): lax.all_to_all(outgoing, 'fsdp', split_axis=0, concat_axis=1, tiled=True)  11.3 us
    all_gather x1, waiting for transfers between devices, body(): lax.all_gather(finish_step(received), 'refresh', axis=0, tiled=True)[:2]  9.82 us
    unnamed x50, local copies, waits for them, and re-layouts  7.11 us
    all_to_all x3, local copies, waits for them, and re-layouts, body(): lax.all_to_all(update.reshape(cap, width * width), 'fsdp', split_axis=1,...  6.99 us
    all_to_all x1, starting transfers between devices, body(): lax.all_to_all(update.reshape(cap, width * width), 'fsdp', split_axis=1,...  6.34 us
  transfers between devices with their start and end apart: 4, of which 3 were waited for; matrix products, arithmetic and copies ran while one was open for 55% of the time, Pallas kernels for 0%

commit v1 on v0

--- a/solution.py
+++ b/solution.py
@@ -5,6 +5,19 @@
 
 HIGHEST = lax.Precision.HIGHEST
 EPSILON = 1e-08
+
+
+def gather_around(shard, axis, dim):
+    ways = lax.axis_size(axis)
+    up = [(d, (d + 1) % ways) for d in range(ways)]
+    down = [(d, (d - 1) % ways) for d in range(ways)]
+    earlier, later = ([shard], [shard])
+    for _ in range(ways // 2):
+        earlier.append(lax.ppermute(earlier[-1], axis, up))
+    for _ in range((ways - 1) // 2):
+        later.append(lax.ppermute(later[-1], axis, down))
+    line = jnp.concatenate([*earlier[::-1], *later[1:]], axis=dim)
+    return jnp.roll(line, (lax.axis_index(axis) - ways // 2) * shard.shape[dim], axis=dim)
 
 
 def split_up(value, dim, length):
@@ -94,7 +107,7 @@
     images_all = jnp.concatenate([image_of(factors, bases), filler], axis=0)
     offered = jnp.where(group == chosen, images_all, jnp.zeros_like(images_all))
     received = sum_at_owner(offered, "refresh", 0)
-    fresh = lax.all_gather(finish_step(received), "refresh", axis=0, tiled=True)[:2]
+    fresh = gather_around(finish_step(received), "refresh", 0)[:2]
     leading = (jnp.arange(cap, dtype=jnp.int32) == 0)[:, None, None]
     refreshed = keep & leading & (group == chosen)
     left_basis_new = jnp.where(refreshed, fresh[0][None], left_turn)

time: 191 us -> 182 us (0.953)
  between operations: 16.5 us -> 3.14 us
  starting transfers between devices: 23.3 us -> 28.8 us
  local copies, waits for them, and re-layouts: 33 us -> 28.9 us
  other arithmetic: 76.1 us -> 80 us
  waiting for transfers between devices: 22.5 us -> 18.7 us
  matrix products: 18.1 us -> 20.6 us
    all_gather x1 -> x0, waiting for transfers between devices: 9.82 us -> none  [body(): lax.all_gather(finish_step(received), 'refresh', axis=0, tiled=True)[:2]]
    ppermute x0 -> x3, waiting for transfers between devices: none -> 8.5 us  [the longest x2 8.13 us: gather_around(): earlier.append(lax.ppermute(earlier[-1], axis, up))]
    ppermute x0 -> x3, starting transfers between devices: none -> 5.17 us  [the longest x1 2.71 us: gather_around(): later.append(lax.ppermute(later[-1], axis, down))]
    unnamed x50 -> x49, local copies, waits for them, and re-layouts: 7.11 us -> 2.12 us
    another operation x3, other arithmetic: 21.1 us -> 23.4 us  [finish_step(): jax.scipy.linalg.solve_triangular(lower, jnp.swapaxes(image, 1, 2), lower...]
    another operation x6, other arithmetic: 36.8 us -> 39 us  [finish_step(): lower = jnp.linalg.cholesky(gram)]
  transfers between devices with their start and end apart: 4 -> 6, of which waited for: 3 -> 4; matrix products, arithmetic and copies ran while one was open for 55% -> 61% of each run, Pallas kernels for 0% -> 0%
where the time goes in v1:
time: 182 us; the launch traced here: 180 us
  other arithmetic  80 us (44%)
  local copies, waits for them, and re-layouts  28.9 us (16%)
  starting transfers between devices  28.8 us (16%)
  matrix products  20.6 us (11%)
  waiting for transfers between devices  18.7 us (10%)
  between operations  3.14 us (2%)
    another operation x6, other arithmetic, finish_step(): lower = jnp.linalg.cholesky(gram)  39 us
    another operation x3, other arithmetic, finish_step(): jax.scipy.linalg.solve_triangular(lower, jnp.swapaxes(image, 1, 2), lower...  23.4 us
    all_to_all x1, starting transfers between devices, body(): lax.all_to_all(outgoing, 'fsdp', split_axis=0, concat_axis=1, tiled=True)  12.1 us
    all_to_all x1, waiting for transfers between devices, body(): lax.all_to_all(outgoing, 'fsdp', split_axis=0, concat_axis=1, tiled=True)  10.2 us
    ppermute x2, waiting for transfers between devices, gather_around(): earlier.append(lax.ppermute(earlier[-1], axis, up))  8.13 us
    another operation x8, local copies, waits for them, and re-layouts  7.19 us
    all_to_all x1, starting transfers between devices, body(): lax.all_to_all(update.reshape(cap, width * width), 'fsdp', split_axis=1,...  7.11 us
    all_to_all x3, local copies, waits for them, and re-layouts, body(): lax.all_to_all(update.reshape(cap, width * width), 'fsdp', split_axis=1,...  6.97 us
  transfers between devices with their start and end apart: 6, of which 4 were waited for; matrix products, arithmetic and copies ran while one was open for 61% of the time, Pallas kernels for 0%

profile of v1, /device:TPU:8, one launch (start us, length us, event | category | flops | bytes accessed | tf_op | source)
XLA Modules:
  0.0 180.1 jit_solution(4900218547110016145)
XLA Ops:
  0.7 0.8 iota_compare_fusion.7
  4.1 1.0 all_to_all.29
  5.1 12.1 %all-to-all-start = ((bf16[64,4,1024]{2,1,0:T(4,128)(2,1)}), bf16[64,4,1024]{2,1,0:T(4,128)(2,1)S(1)}, u32[]{:S(2)}, u32[]{:S(2)}) async-start(bf16[64,4,1024]{2,1,0:T(4,128)(2,1)} %all_to_all.29), calls=%async_computation | async-start | bytes 1048576 | tf_op jit(solution)/shard_map/all_to_all | solution.py:77
  20.4 1.2 and_and_fusion
  23.7 10.2 %all-to-all-done = bf16[64,4,1024]{2,1,0:T(4,128)(2,1)S(1)} async-done(((bf16[64,4,1024]{2,1,0:T(4,128)(2,1)}), bf16[64,4,1024]{2,1,0:T(4,128)(2,1)S(1)}, u32[]{:S(2)}, u32[]{:S(2)}) %all-to-all-start) | async-done | bytes 524320 | tf_op jit(solution)/shard_map/all_to_all | solution.py:77
  33.9 1.0 copy.118
  34.9 1.4 reshape.256
  36.2 2.0 %fusion.17 = f32[4,256,256]{1,2,0:T(8,128)} fusion(bf16[4,256,256]{2,1,0:T(8,128)(2,1)S(1)} %reshape.256, f32[1,4,256,256]{3,2,1,0:T(8,128)S(1)} %copy-done.1), kind=kOutput, calls=%fused_computation.33 | convolution fusion | flops 805306368 | bytes 2621440 | tf_op jit(solution)/shard_map/sji,sjk->sik/dot_general | solution.py:46
  38.7 0.8 copy-done.7
  40.9 1.1 fusion.4
  41.9 4.4 %all-to-all-start.2 = ((f32[4,1,256,256]{3,2,1,0:T(8,128)}), f32[4,1,256,256]{3,2,1,0:T(8,128)}, u32[]{:S(2)}, u32[]{:S(2)}) async-start(f32[4,1,256,256]{3,2,1,0:T(8,128)} %fusion.4), calls=%async_computation.2 | async-start | bytes 2097152 | tf_op jit(solution)/shard_map/all_to_all | solution.py:30
  46.4 3.3 %fusion.19 = f32[4,256,256]{1,2,0:T(8,128)S(1)} fusion(f32[1,4,256,256]{3,2,1,0:T(8,128)S(1)} %copy-done.1, bf16[4,256,256]{2,1,0:T(8,128)(2,1)S(1)} %reshape.256, f32[1,4,256,256]{3,2,1,0:T(8,128)} %param.16), kind=kOutput, calls=%fused_computation.35 | convolution fusion | flops 806354944 | bytes 3670016 | tf_op jit(solution)/shard_map/sji,sjk->sik/dot_general | solution.py:46
  49.7 1.3 fusion.3
  51.0 1.4 convolution_divide_fusion
  52.4 1.2 fusion.15
  53.6 2.1 %fusion.8 = f32[4,256,256]{2,1,0:T(8,128)} fusion(f32[4,256,256]{1,2,0:T(8,128)S(1)} %fusion.15, f32[1,4,256,256]{3,2,1,0:T(8,128)S(1)} %copy-done.2), kind=kOutput, calls=%fused_computation.26 | convolution fusion | flops 805306368 | bytes 3145728 | tf_op jit(solution)/shard_map/sij,skj->sik/dot_general | solution.py:96
  55.7 2.5 %all_to_all.32 = f32[4,64,1024]{2,1,0:T(8,128)} reshape(f32[4,256,256]{2,1,0:T(8,128)} %fusion.8) | data formatting | bytes 2097152 | tf_op jit(solution)/shard_map/all_to_all | solution.py:97
  58.2 2.9 %copy.95 = f32[4,64,1024]{2,0,1:T(4,128)} copy(f32[4,64,1024]{2,1,0:T(8,128)} %all_to_all.32) | data formatting | bytes 2097152 | tf_op jit(solution)/shard_map/all_to_all | solution.py:97
  61.1 1.2 convert_multiply_fusion
  62.3 2.5 %mul.104 = f32[1,4,256,256]{3,2,1,0:T(8,128)} reshape(f32[4,64,1024]{2,1,0:T(8,128)} %convert_multiply_fusion) | data formatting | bytes 2097152 | tf_op jit(solution)/shard_map/mul | solution.py:90
  64.8 7.1 %all-to-all-start.1 = ((f32[4,64,1024]{2,0,1:T(4,128)}), f32[4,64,1024]{2,0,1:T(4,128)}, u32[]{:S(2)}, u32[]{:S(2)}) async-start(f32[4,64,1024]{2,0,1:T(4,128)} %copy.95), calls=%async_computation.1 | async-start | bytes 2097152 | tf_op jit(solution)/shard_map/all_to_all | solution.py:97
  71.9 1.3 reduce_sum.34
  74.7 11.7 %custom-call.17 = f32[1,128,128]{2,1,0:T(8,128)S(1)} custom-call(f32[1,128,128]{2,1,0:T(8,128)S(1)} %cholesky.117), custom_call_target="Cholesky" | custom-call | tf_op jit(solution)/shard_map/jit(cholesky)/cholesky | solution.py:40
  87.8 1.9 %copy.100 = f32[256,256]{0,1:T(8,128)} copy(f32[256,256]{1,0:T(8,128)} %copy-done.10) | data formatting | bytes 524288 | tf_op jit(solution)/shard_map/reduce_sum | solution.py:31
  89.7 11.3 %custom-call.18 = f32[1,1,128,128]{2,3,1,0:T(8,128)} custom-call(f32[1,1,128,128]{3,2,1,0:T(8,128)} %get-tuple-element.39), custom_call_target="InvertDiagBlocksLowerTriangular" | custom-call | tf_op jit(solution)/shard_map/jit(cholesky)/cholesky | solution.py:40
  100.9 1.7 bitcast_dynamic-update-slice_fusion.1
  102.6 1.7 fusion.2
  104.4 13.2 %custom-call.19 = f32[1,128,128]{2,1,0:T(8,128)} custom-call(f32[1,128,128]{2,1,0:T(8,128)} %fusion.2), custom_call_target="Cholesky" | custom-call | tf_op jit(solution)/shard_map/jit(cholesky)/cholesky | solution.py:40
  117.5 1.5 select_reduce_fusion
  121.1 1.7 bitcast_select_fusion.4
  122.7 0.7 triangular_solve.64
  123.5 7.0 %while.1 = (s32[]{:T(128)}, f32[256,256]{1,0:T(8,128)}, s32[2,2]{1,0:T(2,128)S(1)}, f32[2,128,128]{2,1,0:T(8,128)}, s32[]{:T(128)}) while((s32[]{:T(128)}, f32[256,256]{1,0:T(8,128)}, s32[2,2]{1,0:T(2,128)S(1)}, f32[2,128,128]{2,1,0:T(8,128)}, s32[]{:T(128)}) %tuple.33), condition=%wide.while_cond, body=%wide.while_body.sunk | while | flops 2 | bytes 132705 | solution.py:41
  124.1 2.9 %bitcast_dynamic-update-slice_fusion.3 = f32[2,128,128]{2,1,0:T(8,128)} fusion(f32[2,128,128]{2,1,0:T(8,128)} %get-tuple-element.86, s32[]{:T(128)} %get-tuple-element.83, f32[256,256]{1,0:T(8,128)} %get-tuple-element.89, s32[]{:T(128)} %bitcast.162, s32[]{:T(128)} %bitcast.163), kind=kLoop, calls=%fused_computation.1.clone.1 | loop fusion | bytes 132608 | tf_op jit(solution)/shard_map/jit(_solve_triangular)/triangular_solve
  127.6 2.9 %bitcast_dynamic-update-slice_fusion.3 = f32[2,128,128]{2,1,0:T(8,128)} fusion(f32[2,128,128]{2,1,0:T(8,128)} %get-tuple-element.86, s32[]{:T(128)} %get-tuple-element.83, f32[256,256]{1,0:T(8,128)} %get-tuple-element.89, s32[]{:T(128)} %bitcast.162, s32[]{:T(128)} %bitcast.163), kind=kLoop, calls=%fused_computation.1.clone.1 | loop fusion | bytes 132608 | tf_op jit(solution)/shard_map/jit(_solve_triangular)/triangular_solve
  130.5 21.1 %custom-call.20 = f32[2,128,128]{1,2,0:T(8,128)} custom-call(f32[2,128,128]{2,1,0:T(8,128)} %get-tuple-element.14), custom_call_target="InvertDiagBlocksLowerTriangular" | custom-call | tf_op jit(solution)/shard_map/jit(_solve_triangular)/triangular_solve | solution.py:41
  151.6 1.3 fusion.35
  152.9 1.2 convolution_subtract_fusion
  154.2 1.1 fusion.38
  155.4 1.9 %collective-permute-start = (f32[1,256,256]{1,2,0:T(8,128)S(1)}, f32[1,256,256]{1,2,0:T(8,128)S(1)}, u32[]{:S(2)}, u32[]{:S(2)}) collective-permute-start(f32[1,256,256]{1,2,0:T(8,128)S(1)} %maximum_bitcast_fusion), channel_id=1, source_target_pairs={{0,1},{1,2},{2,3},{3,0},{4,5},{5,6},{6,7},{7,4},{8,9},{9,10},{10,1... | collective-permute-start | bytes 786440 | tf_op jit(solution)/shard_map/ppermute | solution.py:16
  157.3 4.0 %fusion.7 = (f32[1,4,256,256]{3,2,1,0:T(8,128)}, f32[1,4,256,256]{3,2,1,0:T(8,128)}, f32[1,4,256,256]{3,2,1,0:T(8,128)}) fusion(f32[4,256,256]{2,1,0:T(8,128)} %copy-done.12, f32[1,4,256,256]{3,2,1,0:T(8,128)} %param.17, pred[4]{0:T(512)(128)(4,1)S(1)} %iota_compare_fusion.9, f32[4,256,256]{2,1,0:T(8,128)S(1)} %copy-done.6, f32[1,4,256,256]{3,2,1,0:T(8,128)} %param.13, ...), kind=kLoop, calls=%fused_computation.25 | loop fusion | flops 786432 | bytes 9437188 | tf_op jit(solution)/shard_map/broadcast_in_dim | solution.py:122
  161.3 3.8 %collective-permute-done = f32[1,256,256]{1,2,0:T(8,128)S(1)} collective-permute-done((f32[1,256,256]{1,2,0:T(8,128)S(1)}, f32[1,256,256]{1,2,0:T(8,128)S(1)}, u32[]{:S(2)}, u32[]{:S(2)}) %collective-permute-start) | collective-permute-done | bytes 262176 | tf_op jit(solution)/shard_map/ppermute | solution.py:16
  165.6 1.2 add_select_fusion
  166.8 2.7 %collective-permute-start.2 = (f32[1,256,256]{1,2,0:T(8,128)S(1)}, f32[1,256,256]{1,2,0:T(8,128)S(1)}, u32[]{:S(2)}, u32[]{:S(2)}) collective-permute-start(f32[1,256,256]{1,2,0:T(8,128)S(1)} %maximum_bitcast_fusion), channel_id=1, source_target_pairs={{0,3},{1,0},{2,1},{3,2},{4,7},{5,4},{6,5},{7,6},{8,11},{9,8},{10,9... | collective-permute-start | bytes 786440 | tf_op jit(solution)/shard_map/ppermute | solution.py:18
  169.5 4.4 %collective-permute-done.1 = f32[1,256,256]{1,2,0:T(8,128)S(1)} collective-permute-done((f32[1,256,256]{1,2,0:T(8,128)S(1)}, f32[1,256,256]{1,2,0:T(8,128)S(1)}, u32[]{:S(2)}, u32[]{:S(2)}) %collective-permute-start.1) | collective-permute-done | bytes 262176 | tf_op jit(solution)/shard_map/ppermute | solution.py:16
  175.0 1.6 broadcast_select_fusion
  176.5 1.6 all_to_all.35
  178.1 0.9 gather_fusion
  179.1 1.0 bitcast_select_fusion.3
  (95 shorter events, 15.3 us)
Async XLA Ops:
  0.6 3.2 %copy-start = (bf16[1,192,1024]{2,1,0:T(8,128)(2,1)S(1)}, bf16[1,192,1024]{2,1,0:T(8,128)(2,1)}, u32[]{:S(2)}) copy-start(bf16[1,192,1024]{2,1,0:T(8,128)(2,1)} %param.9) | copy-start | bytes 1179652
  0.6 17.2 %copy-start.19 = (s32[1,192,1]{1,2,0:T(1,128)S(1)}, s32[1,192,1]{1,2,0:T(1,128)}, u32[]{:S(2)}) copy-start(s32[1,192,1]{1,2,0:T(1,128)} %param.10) | copy-start | bytes 2308
  0.7 17.8 %copy-start.21 = (s32[64]{0:T(128)S(1)}, s32[64]{0:T(128)}, u32[]{:S(2)}) copy-start(s32[64]{0:T(128)} %param.11) | copy-start | bytes 772
  0.7 21.6 %copy-start.2 = (f32[1,4,256,256]{3,2,1,0:T(8,128)S(1)}, f32[1,4,256,256]{3,2,1,0:T(8,128)}, u32[]{:S(2)}) copy-start(f32[1,4,256,256]{3,2,1,0:T(8,128)} %param.15) | copy-start | bytes 3145732
  2.1 20.9 %copy-start.1 = (f32[1,4,256,256]{3,2,1,0:T(8,128)S(1)}, f32[1,4,256,256]{3,2,1,0:T(8,128)}, u32[]{:S(2)}) copy-start(f32[1,4,256,256]{3,2,1,0:T(8,128)} %param.14) | copy-start | bytes 3145732
  5.1 28.8 %all-to-all-start = ((bf16[64,4,1024]{2,1,0:T(4,128)(2,1)}), bf16[64,4,1024]{2,1,0:T(4,128)(2,1)S(1)}, u32[]{:S(2)}, u32[]{:S(2)}) async-start(bf16[64,4,1024]{2,1,0:T(4,128)(2,1)} %all_to_all.29), calls=%async_computation | async-start | bytes 1048576 | tf_op jit(solution)/shard_map/all_to_all | solution.py:77
  36.2 2.0 %copy-start.8 = (f32[1,4,256,256]{3,2,1,0:T(8,128)S(1)}, f32[1,4,256,256]{3,2,1,0:T(8,128)}, u32[]{:S(2)}) copy-start(f32[1,4,256,256]{3,2,1,0:T(8,128)} %param.12) | copy-start | bytes 3145732
  38.3 1.2 copy-start.7
  38.6 1.3 copy-start.3
  38.6 1.3 copy-start.16
  38.6 1.5 copy-start.17
  39.5 1.3 copy-start.15
  39.9 1.0 copy-start.5
  41.9 22.8 %all-to-all-start.2 = ((f32[4,1,256,256]{3,2,1,0:T(8,128)}), f32[4,1,256,256]{3,2,1,0:T(8,128)}, u32[]{:S(2)}, u32[]{:S(2)}) async-start(f32[4,1,256,256]{3,2,1,0:T(8,128)} %fusion.4), calls=%async_computation.2 | async-start | bytes 2097152 | tf_op jit(solution)/shard_map/all_to_all | solution.py:30
  46.4 3.3 %copy-start.11 = (f32[1,4,256,256]{3,2,1,0:T(8,128)S(1)}, f32[1,4,256,256]{3,2,1,0:T(8,128)}, u32[]{:S(2)}) copy-start(f32[1,4,256,256]{3,2,1,0:T(8,128)} %param.17) | copy-start | bytes 3145732
  46.4 3.3 %copy-start.14 = (f32[4,256,256]{1,2,0:T(8,128)S(1)}, f32[4,256,256]{1,2,0:T(8,128)}, u32[]{:S(2)}) copy-start(f32[4,256,256]{1,2,0:T(8,128)} %fusion.17) | copy-start | bytes 3145732
  51.0 1.4 copy-start.12
  64.8 111.8 %all-to-all-start.1 = ((f32[4,64,1024]{2,0,1:T(4,128)}), f32[4,64,1024]{2,0,1:T(4,128)}, u32[]{:S(2)}, u32[]{:S(2)}) async-start(f32[4,64,1024]{2,0,1:T(4,128)} %copy.95), calls=%async_computation.1 | async-start | bytes 2097152 | tf_op jit(solution)/shard_map/all_to_all | solution.py:97
  73.2 13.9 %copy-start.10 = (f32[256,256]{1,0:T(8,128)}, f32[256,256]{1,0:T(8,128)S(1)}, u32[]{:S(2)}) copy-start(f32[256,256]{1,0:T(8,128)S(1)} %reduce_sum.34) | copy-start | bytes 786436
  74.0 0.7 copy-start.18
  87.8 69.5 %copy-start.4 = (f32[4,256,256]{2,1,0:T(8,128)S(1)}, f32[4,256,256]{2,1,0:T(8,128)}, u32[]{:S(2)}) copy-start(f32[4,256,256]{2,1,0:T(8,128)} %copy-done.3) | copy-start | bytes 3145732
  151.6 5.7 %copy-start.6 = (f32[4,256,256]{2,1,0:T(8,128)S(1)}, f32[4,256,256]{2,1,0:T(8,128)}, u32[]{:S(2)}) copy-start(f32[4,256,256]{2,1,0:T(8,128)} %copy-done.5) | copy-start | bytes 3145732
  155.3 10.3 %copy-start.9 = (f32[1,4,256,256]{3,2,1,0:T(8,128)S(1)}, f32[1,4,256,256]{3,2,1,0:T(8,128)}, u32[]{:S(2)}) copy-start(f32[1,4,256,256]{3,2,1,0:T(8,128)} %param.16) | copy-start | bytes 3145732
  155.4 10.3 %copy-start.13 = (f32[1,4,256,256]{3,2,1,0:T(8,128)S(1)}, f32[1,4,256,256]{3,2,1,0:T(8,128)}, u32[]{:S(2)}) copy-start(f32[1,4,256,256]{3,2,1,0:T(8,128)} %mul.104) | copy-start | bytes 3145732
  155.4 9.7 %collective-permute-start = (f32[1,256,256]{1,2,0:T(8,128)S(1)}, f32[1,256,256]{1,2,0:T(8,128)S(1)}, u32[]{:S(2)}, u32[]{:S(2)}) collective-permute-start(f32[1,256,256]{1,2,0:T(8,128)S(1)} %maximum_bitcast_fusion), channel_id=1, source_target_pairs={{0,1},{1,2},{2,3},{3,0},{4,5},{5,6},{6,7},{7,4},{8,9},{9,10},{10,1... | collective-permute-start | bytes 786440 | tf_op jit(solution)/shard_map/ppermute | solution.py:16
  165.1 8.8 %collective-permute-start.1 = (f32[1,256,256]{1,2,0:T(8,128)S(1)}, f32[1,256,256]{1,2,0:T(8,128)S(1)}, u32[]{:S(2)}, u32[]{:S(2)}) collective-permute-start(f32[1,256,256]{1,2,0:T(8,128)S(1)} %collective-permute-done), channel_id=1, source_target_pairs={{0,1},{1,2},{2,3},{3,0},{4,5},{5,6},{6,7},{7,4},{8,9},{9,10},{10,1... | collective-permute-start | bytes 786440 | tf_op jit(solution)/shard_map/ppermute | solution.py:16
  166.8 7.5 %collective-permute-start.2 = (f32[1,256,256]{1,2,0:T(8,128)S(1)}, f32[1,256,256]{1,2,0:T(8,128)S(1)}, u32[]{:S(2)}, u32[]{:S(2)}) collective-permute-start(f32[1,256,256]{1,2,0:T(8,128)S(1)} %maximum_bitcast_fusion), channel_id=1, source_target_pairs={{0,3},{1,0},{2,1},{3,2},{4,7},{5,4},{6,5},{7,6},{8,11},{9,8},{10,9... | collective-permute-start | bytes 786440 | tf_op jit(solution)/shard_map/ppermute | solution.py:18
  174.4 0.6 copy-start.20
